TPU v7x, 256 devices: a whole 4x4x8 slice. The times are simulated.
256 devices in a mesh: strip: 64 (over y, z, core), chan: 4 (over x).
Axes of the slice: x: 4, y: 4, z: 8, core: 2. Of those that a mesh axis runs over, the one named last changes fastest.
Arguments:
- activations: bfloat16 [512, 128, 1280], P('strip', None, 'chan'), may hold values from -17 to 17
- weight: bfloat16 [9, 1280, 1280], P(None, None, 'chan'), may hold values from -0.0546875 to 0.0546875
- gamma: float32 [1280], replicated, may hold values from 0.25 to 1.75
- beta: float32 [1280], replicated, may hold values from -3 to 3
- group_map: int32 [1280], replicated, may hold values from 0 to 31, as said below
- lengths: int32 [64], P('strip'), may hold values from 1 to 8, 384 in all
- stale_edges: bfloat16 [128, 128, 1280], P('strip', None, 'chan'), may hold values from -6 to 6
- stale_mean: float32 [32], replicated, may hold values from -0.5 to 0.5
- stale_square: float32 [32], replicated, may hold values from 1 to 4
- old_mean: float32 [64, 32], P('strip'), may hold values from -0.5 to 0.5
- old_square: float32 [64, 32], P('strip'), may hold values from 0.5 to 6
Outputs:
- upsampled: bfloat16 [1024, 256, 1280], P('strip', None, 'chan')
- new_mean: float32 [32], replicated
- new_square: float32 [32], replicated
Inputs may be any that keep to these rules, and one draw needn't show every extreme that they name: `group_map`: every group has exactly 40 channels. The lengths sum to 384, and some strip uses all 8 rows.
All inputs are finite; a program needn't handle non-finite values. No bound on the sum of `lengths` on one device may be relied on, other than what follows from the above.
Results may differ from a plain program's by a relative error of at most 0.0027.
Values may be sent and summed in bfloat16 or wider, within the bound.
A program may use at most 64 MiB of HBM per device.

v0:
```python
import jax
import jax.numpy as jnp
from jax import lax
from jax.sharding import PartitionSpec as P

EPS = 1e-05


def from_everyone(value, axis):
    copies = jnp.broadcast_to(value, (lax.axis_size(axis), *value.shape))
    return lax.all_to_all(copies, axis, split_axis=0, concat_axis=0, tiled=True)


def over_copies(value, axis):
    return from_everyone(value, axis).sum(axis=0)


def together(arrays, axis):
    ends = [0]
    for a in arrays:
        ends.append(ends[-1] + a.size)
    subtotal = over_copies(jnp.concatenate([a.ravel() for a in arrays]), axis)
    return tuple((subtotal[b:e].reshape(a.shape) for a, b, e in zip(arrays, ends, ends[1:])))


def padded_2(block, sides, width):
    for axis, dim in sides:
        count = lax.axis_size(axis)
        forward = [(i, i + 1) for i in range(count - 1)]
        backward = [(target, source) for source, target in forward]
        low = lax.ppermute(
            lax.slice_in_dim(block, block.shape[dim] - width, None, axis=dim), axis, forward
        )
        high = lax.ppermute(lax.slice_in_dim(block, 0, width, axis=dim), axis, backward)
        block = jnp.concatenate([low, block, high], axis=dim)
    return block


def per_device(
    activations,
    weight,
    gamma,
    beta,
    group_map,
    lengths,
    stale_edges,
    stale_mean,
    stale_square,
    old_mean,
    old_square,
):
    rows, width, local_c = activations.shape
    channels = weight.shape[1]
    groups = stale_mean.shape[0]
    per_group = channels // groups
    offset = lax.axis_index("chan") * local_c
    member = (group_map[:, None] == jnp.arange(groups, dtype=jnp.int32)[None, :]).astype(
        jnp.float32
    )
    local_member = lax.dynamic_slice_in_dim(member, offset, local_c, 0)
    length = lengths[0]
    used = (jnp.arange(rows, dtype=jnp.int32) < length).astype(jnp.float32)[:, None, None]
    values = activations.astype(jnp.float32) * used
    chan_sum = jnp.sum(values, axis=(0, 1))
    chan_sq = jnp.sum(values * values, axis=(0, 1))
    part_one = jnp.sum(chan_sum[:, None] * local_member, axis=0)
    part_two = jnp.sum(chan_sq[:, None] * local_member, axis=0)
    strip_one, strip_two = together((part_one, part_two), "chan")
    total_count = float(lax.axis_size("strip") * (3 * rows // 4) * width * per_group)
    image_one, image_two = together((strip_one, strip_two), "strip")
    new_mean = image_one / total_count
    new_square = image_two / total_count
    count = length.astype(jnp.float32) * (width * per_group)
    fresh_mean = strip_one / count
    fresh_square = strip_two / count
    mean_g = stale_mean + fresh_mean - old_mean[0]
    square_g = stale_square + fresh_square - old_square[0]
    var_g = jnp.maximum(square_g - mean_g * mean_g, 0.5 * (fresh_square - fresh_mean * fresh_mean))
    rstd_g = lax.rsqrt(var_g + EPS)
    scale_c = jnp.sum(member * rstd_g[None, :], axis=1) * gamma
    shift_c = beta - jnp.sum(member * mean_g[None, :], axis=1) * scale_c
    bordered = padded_2(stale_edges, (("strip", 0),), 1)
    bounds = jnp.stack([bordered[0], bordered[3]], axis=0)
    initial = jnp.zeros((rows * width, local_c), jnp.float32)
    total = initial
    piece = lax.all_gather(activations, "chan", axis=2, tiled=True)
    bound = lax.all_gather(bounds, "chan", axis=2, tiled=True)
    depth = piece.shape[2]
    act = (jax.nn.silu(piece.astype(jnp.float32) * scale_c + shift_c) * used).astype(jnp.bfloat16)
    padded = jnp.concatenate([bound[0:1], act, jnp.zeros((1, width, depth), jnp.bfloat16)], axis=0)
    place = (jnp.arange(rows + 2, dtype=jnp.int32) == length + 1)[:, None, None]
    padded = jnp.where(place, bound[1][None], padded)
    padded = jnp.pad(padded, ((0, 0), (1, 1), (0, 0)))
    for tap in range(9):
        down, across = (tap // 3, tap % 3)
        patch = padded[down : down + rows, across : across + width].reshape(rows * width, depth)
        total = total + jnp.dot(patch, weight[tap], preferred_element_type=jnp.float32)
    block = ((activations.astype(jnp.float32) + total.reshape(rows, width, local_c)) * used).astype(
        jnp.bfloat16
    )
    upsampled = jnp.repeat(jnp.repeat(block, 2, axis=0), 2, axis=1)
    return (upsampled, new_mean, new_square)


def solution(mesh):
    in_specs = (
        P("strip", None, "chan"),
        P(None, None, "chan"),
        P(),
        P(),
        P(),
        P("strip"),
        P("strip", None, "chan"),
        P(),
        P(),
        P("strip", None),
        P("strip", None),
    )
    out_specs = (P("strip", None, "chan"), P(), P())
    return jax.shard_map(
        per_device, mesh=mesh, in_specs=in_specs, out_specs=out_specs, check_vma=False
    )
```

profile of v0, /device:TPU:2, one launch (start us, length us, event | category | flops | bytes accessed | tf_op | source)
XLA Modules:
  0.0 105.8 jit_solution(1750470864157832420)
XLA Ops:
  7.2 0.0 all-gather.2.cloned.1.call-start
  7.3 2.4 %copy.58 = bf16[8,128,320]{1,0,2:T(8,128)(2,1)} copy(bf16[8,128,320]{1,2,0:T(8,128)(2,1)} %param.11) | data formatting | bytes 1310720 | tf_op args[0]
  9.7 0.0 all-gather.2.cloned.1.call-update
  10.4 1.4 %fusion.1 = (f32[320]{0:T(512)S(1)}, f32[320]{0:T(512)S(1)}) fusion(bf16[8,128,320]{1,2,0:T(8,128)(2,1)} %param.11, f32[8]{0:T(128)S(1)} %compare_convert_fusion), kind=kLoop, calls=%fused_computation.11 | loop fusion | flops 1637760 | bytes 657952 | tf_op jit(solution)/shard_map/reduce_sum | solution.py:64
  11.9 0.2 fusion.26
  12.1 0.1 pad_maximum_fusion.1
  12.2 0.6 broadcast_in_dim.46
  12.7 5.4 %all-to-all-start = ((f32[4,1,64]{2,1,0:T(1,128)}), f32[4,1,64]{2,1,0:T(1,128)S(1)}, u32[]{:S(2)}, u32[]{:S(2)}) async-start(f32[4,1,64]{2,1,0:T(1,128)} %broadcast_in_dim.46), calls=%async_computation | async-start | bytes 4096 | tf_op jit(solution)/shard_map/all_to_all | solution.py:11
  18.2 0.1 copy.65
  18.3 1.3 %collective-permute-start = (bf16[1,128,320]{1,0,2:T(2,128)(2,1)S(1)}, bf16[1,128,320]{1,0,2:T(2,128)(2,1)S(1)}, u32[]{:S(2)}, u32[]{:S(2)}) collective-permute-start(bf16[1,128,320]{1,0,2:T(2,128)(2,1)S(1)} %copy.65), channel_id=1, source_target_pairs={{0,4},{4,8},{8,12},{12,16},{16,20},{20,24},{24,28},{28,32},{32,36}... | collective-permute-start | bytes 245768 | tf_op jit(solution)/shard_map/ppermute | solution.py:31
  19.6 0.1 copy.66
  19.8 1.3 %collective-permute-start.1 = (bf16[1,128,320]{1,0,2:T(2,128)(2,1)S(1)}, bf16[1,128,320]{1,0,2:T(2,128)(2,1)S(1)}, u32[]{:S(2)}, u32[]{:S(2)}) collective-permute-start(bf16[1,128,320]{1,0,2:T(2,128)(2,1)S(1)} %copy.66), channel_id=1, source_target_pairs={{4,0},{8,4},{12,8},{16,12},{20,16},{24,20},{28,24},{32,28},{36,32}... | collective-permute-start | bytes 245768 | tf_op jit(solution)/shard_map/ppermute | solution.py:34
  21.1 0.1 pad.7.clone
  21.2 0.8 all-to-all-done
  22.0 0.6 broadcast_in_dim.50
  22.7 14.8 %all-to-all-start.1 = ((f32[64,1,64]{2,1,0:T(1,128)}), f32[64,1,64]{2,1,0:T(1,128)S(1)}, u32[]{:S(2)}, u32[]{:S(2)}) async-start(f32[64,1,64]{2,1,0:T(1,128)} %broadcast_in_dim.50), calls=%async_computation.1 | async-start | bytes 65536 | tf_op jit(solution)/shard_map/all_to_all | solution.py:11
  37.5 0.1 add_rsqrt_fusion
  37.6 0.1 select_reduce_fusion.1
  37.8 9.2 %all-to-all-done.1 = f32[64,1,64]{2,1,0:T(1,128)S(1)} async-done(((f32[64,1,64]{2,1,0:T(1,128)}), f32[64,1,64]{2,1,0:T(1,128)S(1)}, u32[]{:S(2)}, u32[]{:S(2)}) %all-to-all-start.1) | async-done | bytes 16416 | tf_op jit(solution)/shard_map/all_to_all | solution.py:11
  47.1 0.6 slice_multiply_fusion
  47.6 0.4 pad_maximum_fusion
  48.0 13.7 %all_gather.6 = bf16[2,128,1280]{1,0,2:T(2,128)(2,1)S(1)} all-gather(bf16[2,128,320]{1,0,2:T(2,128)(2,1)S(1)} %pad_maximum_fusion), channel_id=1, replica_groups=mesh['strip'=64,'chan'=4] {'chan'}, dimensions={2}, use_global_device_ids=true | all-gather | bytes 819200 | tf_op jit(solution)/shard_map/all_gather | solution.py:87
  61.7 0.9 fusion.29
  62.6 0.5 copy.67
  63.1 0.5 copy.68
  63.5 0.0 all-gather.2.cloned.1.call-done
  63.6 3.8 %copy.59 = bf16[8,128,1280]{2,1,0:T(8,128)(2,1)S(1)} copy(bf16[8,128,1280]{1,0,2:T(8,128)(2,1)} %all-gather.2.cloned.1.call-done) | data formatting | bytes 5242880 | tf_op jit(solution)/shard_map/all_gather | solution.py:86
  67.4 1.7 %multiply_convert_fusion = bf16[8,128,1280]{2,1,0:T(8,128)(2,1)S(1)} fusion(bf16[8,128,1280]{2,1,0:T(8,128)(2,1)S(1)} %copy.59, f32[8]{0:T(128)S(1)} %compare_convert_fusion, f32[1280]{0:T(1024)S(1)} %get-tuple-element.27, f32[1280]{0:T(1024)S(1)} %get-tuple-element.28), kind=kLoop, calls=%fused_computation | loop fusion | flops 11796480 | bytes 5253152 | tf_op jit(solution)/shard_map/convert_element_type | solution.py:89
  69.1 0.5 maximum_select_fusion
  69.5 10.1 %pad_slice_fusion = (bf16[8,128,1280]{2,1,0:T(8,128)(2,1)S(1)}, bf16[8,128,1280]{2,1,0:T(8,128)(2,1)S(1)}, bf16[8,128,1280]{2,1,0:T(8,128)(2,1)S(1)}, bf16[8,128...) fusion(bf16[10,128,1280]{2,1,0:T(8,128)(2,1)S(1)} %maximum_sele, ...), kind=kLoop, calls=%fused_computation.2 | loop fusion | bytes 34734080 | tf_op jit(solution)/shard_map/slice | solution.py:96
  79.6 0.0 slice-start
  79.6 2.3 %fusion.14 = f32[1024,320]{0,1:T(8,128)S(1)} fusion(bf16[1024,1280]{1,0:T(8,128)(2,1)S(1)} %bitcast.80, bf16[9,1280,320]{1,2,0:T(8,128)(2,1)} %param.12), kind=kOutput, calls=%fused_computation.32 | convolution fusion | flops 838860800 | bytes 4751360 | tf_op jit(solution)/shard_map/dot_general | solution.py:97
  82.0 0.0 slice-start.1
  82.0 2.4 %convolution_add_fusion.7 = f32[1024,320]{0,1:T(8,128)S(1)} fusion(f32[1024,320]{0,1:T(8,128)S(1)} %fusion.14, bf16[1024,1280]{1,0:T(8,128)(2,1)S(1)} %bitcast.79, bf16[9,1280,320]{1,2,0:T(8,128)(2,1)} %param.12), kind=kOutput, calls=%fused_computation.20 | convolution fusion | flops 839188480 | bytes 6062080 | tf_op jit(solution)/shard_map/dot_general | solution.py:97
  84.4 1.1 convolution_add_fusion.6
  85.4 1.1 convolution_add_fusion.5
  86.5 1.1 convolution_add_fusion.4
  87.5 1.1 convolution_add_fusion.3
  88.6 1.1 convolution_add_fusion.2
  89.7 1.1 convolution_add_fusion.1
  90.7 0.0 copy-start
  90.7 1.1 fusion.2
  91.8 0.0 copy-done
  91.8 0.2 fusion.5
  92.0 0.2 broadcast_in_dim.48
  92.3 1.9 %copy.62 = bf16[16,128,320]{2,0,1:T(8,128)(2,1)} copy(bf16[16,128,320]{1,2,0:T(8,128)(2,1)S(1)} %bitcast.71) | data formatting | bytes 2621440 | tf_op jit(solution)/shard_map/reshape | solution.py:101
  94.2 1.7 %broadcast_in_dim.49 = bf16[16,128,2,320]{3,0,2,1:T(8,128)(2,1)S(1)} broadcast(bf16[16,128,320]{2,0,1:T(8,128)(2,1)} %copy.62), dimensions={0,1,3} | broadcast | bytes 3932160 | tf_op jit(solution)/shard_map/broadcast_in_dim | solution.py:101
  95.8 3.1 %copy.64 = bf16[16,256,320]{1,2,0:T(8,128)(2,1)} copy(bf16[16,256,320]{2,0,1:T(8,128)(2,1)S(1)} %bitcast.70) | data formatting | bytes 5242880
  (28 shorter events, 0.1 us)
Async XLA Ops:
  7.2 4.7 %copy-start.2 = (s32[1280]{0:T(1024)S(1)}, s32[1280]{0:T(1024)}, u32[]{:S(2)}) copy-start(s32[1280]{0:T(1024)} %param.15) | copy-start | bytes 15364
  7.2 11.0 %copy-start.1 = (bf16[2,128,320]{1,2,0:T(8,128)(2,1)S(1)}, bf16[2,128,320]{1,2,0:T(8,128)(2,1)}, u32[]{:S(2)}) copy-start(bf16[2,128,320]{1,2,0:T(8,128)(2,1)} %param.17) | copy-start | bytes 491524
  7.2 30.3 %copy-start.8 = (f32[32]{0:T(128)S(1)}, f32[32]{0:T(128)}, u32[]{:S(2)}) copy-start(f32[32]{0:T(128)} %param.18) | copy-start | bytes 388
  7.2 30.3 %copy-start.6 = (f32[32]{0:T(128)S(1)}, f32[32]{0:T(128)}, u32[]{:S(2)}) copy-start(f32[32]{0:T(128)} %param.19) | copy-start | bytes 388
  7.2 30.3 %copy-start.7 = (f32[1,32]{1,0:T(1,128)S(1)}, f32[1,32]{1,0:T(1,128)}, u32[]{:S(2)}) copy-start(f32[1,32]{1,0:T(1,128)} %param.20) | copy-start | bytes 388
  7.2 30.3 %copy-start.5 = (f32[1,32]{1,0:T(1,128)S(1)}, f32[1,32]{1,0:T(1,128)}, u32[]{:S(2)}) copy-start(f32[1,32]{1,0:T(1,128)} %param.21) | copy-start | bytes 388
  7.2 30.5 %copy-start.4 = (f32[1280]{0:T(1024)S(1)}, f32[1280]{0:T(1024)}, u32[]{:S(2)}) copy-start(f32[1280]{0:T(1024)} %param.13) | copy-start | bytes 15364
  7.2 30.5 %copy-start.3 = (f32[1280]{0:T(1024)S(1)}, f32[1280]{0:T(1024)}, u32[]{:S(2)}) copy-start(f32[1280]{0:T(1024)} %param.14) | copy-start | bytes 15364
  7.2 56.3 %all-gather.2.cloned.1.call-start = ((), (), s32[]{:S(2)}) async-start(), calls=%async_computation.2 | async-start | bytes 3276800 | tf_op jit(solution)/shard_map/all_gather | solution.py:86
  12.7 9.3 %all-to-all-start = ((f32[4,1,64]{2,1,0:T(1,128)}), f32[4,1,64]{2,1,0:T(1,128)S(1)}, u32[]{:S(2)}, u32[]{:S(2)}) async-start(f32[4,1,64]{2,1,0:T(1,128)} %broadcast_in_dim.46), calls=%async_computation | async-start | bytes 4096 | tf_op jit(solution)/shard_map/all_to_all | solution.py:11
  18.3 29.3 %collective-permute-start = (bf16[1,128,320]{1,0,2:T(2,128)(2,1)S(1)}, bf16[1,128,320]{1,0,2:T(2,128)(2,1)S(1)}, u32[]{:S(2)}, u32[]{:S(2)}) collective-permute-start(bf16[1,128,320]{1,0,2:T(2,128)(2,1)S(1)} %copy.65), channel_id=1, source_target_pairs={{0,4},{4,8},{8,12},{12,16},{16,20},{20,24},{24,28},{28,32},{32,36}... | collective-permute-start | bytes 245768 | tf_op jit(solution)/shard_map/ppermute | solution.py:31
  19.8 27.9 %collective-permute-start.1 = (bf16[1,128,320]{1,0,2:T(2,128)(2,1)S(1)}, bf16[1,128,320]{1,0,2:T(2,128)(2,1)S(1)}, u32[]{:S(2)}, u32[]{:S(2)}) collective-permute-start(bf16[1,128,320]{1,0,2:T(2,128)(2,1)S(1)} %copy.66), channel_id=1, source_target_pairs={{4,0},{8,4},{12,8},{16,12},{20,16},{24,20},{28,24},{32,28},{36,32}... | collective-permute-start | bytes 245768 | tf_op jit(solution)/shard_map/ppermute | solution.py:34
  22.7 24.4 %all-to-all-start.1 = ((f32[64,1,64]{2,1,0:T(1,128)}), f32[64,1,64]{2,1,0:T(1,128)S(1)}, u32[]{:S(2)}, u32[]{:S(2)}) async-start(f32[64,1,64]{2,1,0:T(1,128)} %broadcast_in_dim.50), calls=%async_computation.1 | async-start | bytes 65536 | tf_op jit(solution)/shard_map/all_to_all | solution.py:11
  79.6 4.7 %slice-start = ((s8[7372800]{0:T(1024)(128)(4,1)}), s8[4194304]{0:T(1024)(128)(4,1)S(1)}, s32[]{:S(2)}) async-start(s8[7372800]{0:T(1024)(128)(4,1)} %bitcast.84), calls=%async_computation.3 | async-start | bytes 8388608
  82.0 2.4 %slice-start.1 = ((s8[7372800]{0:T(1024)(128)(4,1)}), s8[3178496]{0:T(1024)(128)(4,1)S(1)}, s32[]{:S(2)}) async-start(s8[7372800]{0:T(1024)(128)(4,1)} %bitcast.84), calls=%async_computation.4 | async-start | bytes 6356992
  90.7 1.1 %copy-start = (bf16[8,128,320]{1,2,0:T(8,128)(2,1)S(1)}, bf16[8,128,320]{1,2,0:T(8,128)(2,1)}, u32[]{:S(2)}) copy-start(bf16[8,128,320]{1,2,0:T(8,128)(2,1)} %param.11) | copy-start | bytes 1966084
Sparse Core Ops, SparseCore 0:
  10.4 39.7 all-gather.1
where the time goes:
time: 106 us
  local copies, waits for them, and re-layouts  26.7 us (25%)
  starting transfers between devices  22.9 us (22%)
  between operations  15.1 us (14%)
  blocking collectives  13.7 us (13%)
  matrix products  12.1 us (11%)
  waiting for transfers between devices  10.1 us (10%)
  other arithmetic  5.3 us (5%)
    all_to_all x2, starting transfers between devices, from_everyone(): return lax.all_to_all(copies, axis, split_axis=0, concat_axis=0, tiled=True)  20.3 us
    all_gather x1, blocking collectives, per_device(): bound = lax.all_gather(bounds, 'chan', axis=2, tiled=True)  13.7 us
    dot_general x9, matrix products, per_device(): jnp.dot(patch, weight[tap], preferred_element_type=jnp.float32)  12.1 us
    all_to_all x2, waiting for transfers between devices, from_everyone(): return lax.all_to_all(copies, axis, split_axis=0, concat_axis=0, tiled=True)  10.1 us
    slice x1, local copies, waits for them, and re-layouts, per_device(): padded[down:down + rows, across:across + width].reshape(rows * width, depth)  10.1 us
    unnamed x28, local copies, waits for them, and re-layouts  6.78 us
    all_gather x1, local copies, waits for them, and re-layouts, per_device(): piece = lax.all_gather(activations, 'chan', axis=2, tiled=True)  3.83 us
  transfers between devices with their start and end apart: 5, of which 2 were waited for; matrix products, arithmetic and copies ran while one was open for 6% of the time, Pallas kernels for 0%

commit v1 on v0

--- a/solution.py
+++ b/solution.py
@@ -1,9 +1,36 @@
+import functools
 import jax
 import jax.numpy as jnp
 from jax import lax
 from jax.sharding import PartitionSpec as P
 
 EPS = 1e-05
+
+
+def _shape_panel(xin, dim_k):
+    z1 = list(xin.shape[1:])
+    z1[dim_k] *= xin.shape[0]
+    a_next = jnp.moveaxis(xin, 0, dim_k).reshape(z1)
+    return a_next
+
+
+def follow_goods_here(t0, device_axis):
+    earlier, t1 = (lax.axis_size(device_axis), lax.axis_index(device_axis))
+    formed, left_arr = (t0[None], 1)
+    while left_arr < earlier:
+        z = lax.ppermute(formed, device_axis, [(m, m ^ left_arr) for m in range(earlier)])
+        outer = t1 & left_arr == 0
+        formed = jnp.concatenate([jnp.where(outer, formed, z), jnp.where(outer, z, formed)])
+        left_arr *= 2
+    return formed
+
+
+def note_chunk_now(block_here, mat, dim_at):
+    value_now = _shape_panel(follow_goods_here(block_here, mat), dim_at)
+    return value_now
+
+
+list_the_results = functools.partial(note_chunk_now, mat="chan", dim_at=2)
 
 
 def from_everyone(value, axis):
@@ -84,7 +111,7 @@
     initial = jnp.zeros((rows * width, local_c), jnp.float32)
     total = initial
     piece = lax.all_gather(activations, "chan", axis=2, tiled=True)
-    bound = lax.all_gather(bounds, "chan", axis=2, tiled=True)
+    bound = list_the_results(bounds)
     depth = piece.shape[2]
     act = (jax.nn.silu(piece.astype(jnp.float32) * scale_c + shift_c) * used).astype(jnp.bfloat16)
     padded = jnp.concatenate([bound[0:1], act, jnp.zeros((1, width, depth), jnp.bfloat16)], axis=0)

time: 106 us -> 106 us (level); the launches traced: 106 us -> 104 us
  blocking collectives: 13.7 us -> 0 us
  waiting for transfers between devices: 10.1 us -> 21.6 us
  starting transfers between devices: 22.9 us -> 24.9 us
  local copies, waits for them, and re-layouts: 26.7 us -> 25.3 us
    ppermute x0 -> x2, waiting for transfers between devices: none -> 20.5 us  [follow_goods_here(): lax.ppermute(formed, device_axis, [(m, m ^ left_arr) for m in range(earli...]
    all_gather x1 -> x0, blocking collectives: 13.7 us -> none  [per_device(): bound = lax.all_gather(bounds, 'chan', axis=2, tiled=True)]
    all_to_all x2, waiting for transfers between devices: 10.1 us -> 1.11 us  [from_everyone(): return lax.all_to_all(copies, axis, split_axis=0, concat_axis=0, tiled=True)]
    ppermute x0 -> x2, starting transfers between devices: none -> 2.25 us  [follow_goods_here(): lax.ppermute(formed, device_axis, [(m, m ^ left_arr) for m in range(earli...]
    unnamed x28 -> x24, local copies, waits for them, and re-layouts: 6.78 us -> 5.69 us
  transfers between devices with their start and end apart: 5 -> 7, of which waited for: 2 -> 3; matrix products, arithmetic and copies ran while one was open for 6% -> 4% of each run, Pallas kernels for 0% -> 0%
where the time goes in v1:
time: 106 us; the launch traced here: 104 us
  local copies, waits for them, and re-layouts  25.3 us (24%)
  starting transfers between devices  24.9 us (23%)
  waiting for transfers between devices  21.6 us (20%)
  between operations  15.1 us (14%)
  matrix products  12 us (11%)
  other arithmetic  5.09 us (5%)
    ppermute x2, waiting for transfers between devices, follow_goods_here(): lax.ppermute(formed, device_axis, [(m, m ^ left_arr) for m in range(earli...  20.5 us
    all_to_all x2, starting transfers between devices, from_everyone(): return lax.all_to_all(copies, axis, split_axis=0, concat_axis=0, tiled=True)  20 us
    dot_general x9, matrix products, per_device(): jnp.dot(patch, weight[tap], preferred_element_type=jnp.float32)  12 us
    slice x1, local copies, waits for them, and re-layouts, per_device(): padded[down:down + rows, across:across + width].reshape(rows * width, depth)  10 us
    unnamed x24, local copies, waits for them, and re-layouts  5.69 us
    all_gather x1, local copies, waits for them, and re-layouts, per_device(): piece = lax.all_gather(activations, 'chan', axis=2, tiled=True)  4.01 us
    ppermute x2, starting transfers between devices, follow_goods_here(): lax.ppermute(formed, device_axis, [(m, m ^ left_arr) for m in range(earli...  2.25 us
  transfers between devices with their start and end apart: 7, of which 3 were waited for; matrix products, arithmetic and copies ran while one was open for 4% of the time, Pallas kernels for 0%

profile of v1, /device:TPU:2, one launch (start us, length us, event | category | flops | bytes accessed | tf_op | source)
XLA Modules:
  0.0 104.0 jit_solution(6800328070437602725)
XLA Ops:
  7.2 0.0 all-gather.2.cloned.1.call-start
  7.3 2.4 %copy.42 = bf16[8,128,320]{1,0,2:T(8,128)(2,1)} copy(bf16[8,128,320]{1,2,0:T(8,128)(2,1)} %param.11) | data formatting | bytes 1310720 | tf_op args[0]
  9.7 0.0 all-gather.2.cloned.1.call-update
  10.4 1.4 %fusion.1 = (f32[320]{0:T(512)S(1)}, f32[320]{0:T(512)S(1)}) fusion(bf16[8,128,320]{1,2,0:T(8,128)(2,1)} %param.11, f32[8]{0:T(128)S(1)} %compare_convert_fusion), kind=kLoop, calls=%fused_computation.11 | loop fusion | flops 1637760 | bytes 657952 | tf_op jit(solution)/shard_map/reduce_sum | solution.py:91
  11.9 0.2 fusion.26
  12.1 0.1 pad_maximum_fusion.1
  12.2 0.6 broadcast_in_dim.50
  12.8 5.4 %all-to-all-start = ((f32[4,1,64]{2,1,0:T(1,128)}), f32[4,1,64]{2,1,0:T(1,128)S(1)}, u32[]{:S(2)}, u32[]{:S(2)}) async-start(f32[4,1,64]{2,1,0:T(1,128)} %broadcast_in_dim.50), calls=%async_computation | async-start | bytes 4096 | tf_op jit(solution)/shard_map/all_to_all | solution.py:38
  18.2 1.3 %collective-permute-start = (bf16[1,128,320]{1,2,0:T(8,128)(2,1)S(1)}, bf16[1,128,320]{1,2,0:T(8,128)(2,1)S(1)}, u32[]{:S(2)}, u32[]{:S(2)}) collective-permute-start(bf16[1,128,320]{1,2,0:T(8,128)(2,1)S(1)} %get-tuple-element.43), channel_id=1, source_target_pairs={{0,4},{4,8},{8,12},{12,16},{16,20},{20,24},{24,28},{28,32},{32,36}... | collective-permute-start | bytes 245768 | tf_op jit(solution)/shard_map/ppermute | solution.py:58
  19.5 1.3 %collective-permute-start.1 = (bf16[1,128,320]{1,2,0:T(8,128)(2,1)S(1)}, bf16[1,128,320]{1,2,0:T(8,128)(2,1)S(1)}, u32[]{:S(2)}, u32[]{:S(2)}) collective-permute-start(bf16[1,128,320]{1,2,0:T(8,128)(2,1)S(1)} %get-tuple-element.44), channel_id=1, source_target_pairs={{4,0},{8,4},{12,8},{16,12},{20,16},{24,20},{28,24},{32,28},{36,32}... | collective-permute-start | bytes 245768 | tf_op jit(solution)/shard_map/ppermute | solution.py:61
  20.8 0.1 pad.7.clone
  20.9 1.1 %all-to-all-done = f32[4,1,64]{2,1,0:T(1,128)S(1)} async-done(((f32[4,1,64]{2,1,0:T(1,128)}), f32[4,1,64]{2,1,0:T(1,128)S(1)}, u32[]{:S(2)}, u32[]{:S(2)}) %all-to-all-start) | async-done | bytes 1056 | tf_op jit(solution)/shard_map/all_to_all | solution.py:38
  22.0 0.6 broadcast_in_dim.54
  22.7 14.6 %all-to-all-start.1 = ((f32[64,1,64]{2,1,0:T(1,128)}), f32[64,1,64]{2,1,0:T(1,128)S(1)}, u32[]{:S(2)}, u32[]{:S(2)}) async-start(f32[64,1,64]{2,1,0:T(1,128)} %broadcast_in_dim.54), calls=%async_computation.1 | async-start | bytes 65536 | tf_op jit(solution)/shard_map/all_to_all | solution.py:38
  37.3 0.1 collective-permute-start.2
  37.5 0.1 add_rsqrt_fusion
  37.5 0.1 select_reduce_fusion.1
  37.7 10.1 %collective-permute-done.2 = bf16[1,2,128,320]{2,3,0,1:T(8,128)(2,1)S(1)} collective-permute-done((bf16[1,2,128,320]{2,3,0,1:T(8,128)(2,1)S(1)}, bf16[1,2,128,320]{2,3,0,1:T(8,128)(2,1)S(1)}, u32[]{:S(2)}, u32[]{:S(2)}) %collective-permute-start.2) | collective-permute-done | bytes 163872 | tf_op jit(solution)/shard_map/ppermute | solution.py:21
  47.8 2.2 %collective-permute-start.3 = (bf16[2,2,128,320]{2,3,0,1:T(8,128)(2,1)S(1)}, bf16[2,2,128,320]{2,3,0,1:T(8,128)(2,1)S(1)}, u32[]{:S(2)}, u32[]{:S(2)}) collective-permute-start(bf16[2,2,128,320]{2,3,0,1:T(8,128)(2,1)S(1)} %pad_maximum_fusion), channel_id=1, source_target_pairs={{0,2},{1,3},{2,0},{3,1},{4,6},{5,7},{6,4},{7,5},{8,10},{9,11},{10,... | collective-permute-start | bytes 983048 | tf_op jit(solution)/shard_map/ppermute | solution.py:21
  50.0 0.6 slice_multiply_fusion
  50.6 10.4 %collective-permute-done.3 = bf16[2,2,128,320]{2,3,0,1:T(8,128)(2,1)S(1)} collective-permute-done((bf16[2,2,128,320]{2,3,0,1:T(8,128)(2,1)S(1)}, bf16[2,2,128,320]{2,3,0,1:T(8,128)(2,1)S(1)}, u32[]{:S(2)}, u32[]{:S(2)}) %collective-permute-start.3) | collective-permute-done | bytes 327712 | tf_op jit(solution)/shard_map/ppermute | solution.py:21
  61.1 0.1 maximum_bitcast_fusion
  61.2 0.2 copy.41
  61.4 0.2 copy.45
  61.6 0.0 all-gather.2.cloned.1.call-done
  61.6 4.0 %copy.43 = bf16[8,128,1280]{2,1,0:T(8,128)(2,1)S(1)} copy(bf16[8,128,1280]{1,0,2:T(8,128)(2,1)} %all-gather.2.cloned.1.call-done) | data formatting | bytes 5242880 | tf_op jit(solution)/shard_map/all_gather | solution.py:113
  65.6 1.7 %multiply_convert_fusion = bf16[8,128,1280]{2,1,0:T(8,128)(2,1)S(1)} fusion(bf16[8,128,1280]{2,1,0:T(8,128)(2,1)S(1)} %copy.43, f32[8]{0:T(128)S(1)} %compare_convert_fusion, f32[1280]{0:T(1024)S(1)} %get-tuple-element.24, f32[1280]{0:T(1024)S(1)} %get-tuple-element.25), kind=kLoop, calls=%fused_computation | loop fusion | flops 11796480 | bytes 5253152 | tf_op jit(solution)/shard_map/convert_element_type | solution.py:116
  67.3 0.4 maximum_select_fusion
  67.7 10.0 %pad_slice_fusion = (bf16[8,128,1280]{2,1,0:T(8,128)(2,1)S(1)}, bf16[8,128,1280]{2,1,0:T(8,128)(2,1)S(1)}, bf16[8,128,1280]{2,1,0:T(8,128)(2,1)S(1)}, bf16[8,128...) fusion(bf16[10,128,1280]{2,1,0:T(8,128)(2,1)S(1)} %maximum_sele, ...), kind=kLoop, calls=%fused_computation.2 | loop fusion | bytes 34734080 | tf_op jit(solution)/shard_map/slice | solution.py:123
  77.8 0.0 slice-start
  77.8 2.3 %fusion.14 = f32[1024,320]{0,1:T(8,128)S(1)} fusion(bf16[1024,1280]{1,0:T(8,128)(2,1)S(1)} %bitcast.89, bf16[9,1280,320]{1,2,0:T(8,128)(2,1)} %param.12), kind=kOutput, calls=%fused_computation.32 | convolution fusion | flops 838860800 | bytes 4751360 | tf_op jit(solution)/shard_map/dot_general | solution.py:124
  80.1 0.0 slice-start.1
  80.2 2.3 %convolution_add_fusion.7 = f32[1024,320]{0,1:T(8,128)S(1)} fusion(f32[1024,320]{0,1:T(8,128)S(1)} %fusion.14, bf16[1024,1280]{1,0:T(8,128)(2,1)S(1)} %bitcast.88, bf16[9,1280,320]{1,2,0:T(8,128)(2,1)} %param.12), kind=kOutput, calls=%fused_computation.20 | convolution fusion | flops 839188480 | bytes 6062080 | tf_op jit(solution)/shard_map/dot_general | solution.py:124
  82.5 0.1 slice-done.1
  82.6 1.0 %convolution_add_fusion.6 = f32[1024,320]{0,1:T(8,128)S(1)} fusion(f32[1024,320]{0,1:T(8,128)S(1)} %convolution_add_fusion.7, bf16[1024,1280]{1,0:T(8,128)(2,1)S(1)} %bitcast.87, bf16[9,1280,320]{1,2,0:T(8,128)(2,1)S(1)} %bitcast.95), kind=kOutput, calls=%fused_computation.19 | convolution fusion | flops 839188480 | bytes 6062080 | tf_op jit(solution)/shard_map/dot_general | solution.py:124
  83.6 1.0 convolution_add_fusion.5
  84.7 1.0 %convolution_add_fusion.4 = f32[1024,320]{0,1:T(8,128)S(1)} fusion(f32[1024,320]{0,1:T(8,128)S(1)} %convolution_add_fusion.5, bf16[1024,1280]{1,0:T(8,128)(2,1)S(1)} %bitcast.85, bf16[9,1280,320]{1,2,0:T(8,128)(2,1)S(1)} %bitcast.95), kind=kOutput, calls=%fused_computation.17 | convolution fusion | flops 839188480 | bytes 6062080 | tf_op jit(solution)/shard_map/dot_general | solution.py:124
  85.7 1.0 %convolution_add_fusion.3 = f32[1024,320]{0,1:T(8,128)S(1)} fusion(f32[1024,320]{0,1:T(8,128)S(1)} %convolution_add_fusion.4, bf16[1024,1280]{1,0:T(8,128)(2,1)S(1)} %bitcast.84, bf16[9,1280,320]{1,2,0:T(8,128)(2,1)S(1)} %bitcast.95), kind=kOutput, calls=%fused_computation.16 | convolution fusion | flops 839188480 | bytes 6062080 | tf_op jit(solution)/shard_map/dot_general | solution.py:124
  86.8 1.0 convolution_add_fusion.2
  87.8 1.0 %convolution_add_fusion.1 = f32[1024,320]{0,1:T(8,128)S(1)} fusion(f32[1024,320]{0,1:T(8,128)S(1)} %convolution_add_fusion.2, bf16[1024,1280]{1,0:T(8,128)(2,1)S(1)} %bitcast.82, bf16[9,1280,320]{1,2,0:T(8,128)(2,1)S(1)} %bitcast.95), kind=kOutput, calls=%fused_computation.14 | convolution fusion | flops 839188480 | bytes 6062080 | tf_op jit(solution)/shard_map/dot_general | solution.py:124
  88.9 0.0 copy-start
  88.9 1.0 %fusion.2 = f32[40,8,8,128]{3,2,1,0:T(8,128)S(1)} fusion(f32[1024,320]{0,1:T(8,128)S(1)} %convolution_add_fusion.1, bf16[1024,1280]{1,0:T(8,128)(2,1)S(1)} %bitcast.81, bf16[9,1280,320]{1,2,0:T(8,128)(2,1)S(1)} %bitcast.95), kind=kOutput, calls=%fused_computation.13 | convolution fusion | flops 839188480 | bytes 6062080 | tf_op jit(solution)/shard_map/dot_general | solution.py:124
  89.9 0.0 copy-done
  90.0 0.2 fusion.5
  90.2 0.2 broadcast_in_dim.52
  90.4 1.9 %copy.47 = bf16[16,128,320]{2,0,1:T(8,128)(2,1)} copy(bf16[16,128,320]{1,2,0:T(8,128)(2,1)S(1)} %bitcast.80) | data formatting | bytes 2621440 | tf_op jit(solution)/shard_map/reshape | solution.py:128
  92.3 1.7 %broadcast_in_dim.53 = bf16[16,128,2,320]{3,0,2,1:T(8,128)(2,1)S(1)} broadcast(bf16[16,128,320]{2,0,1:T(8,128)(2,1)} %copy.47), dimensions={0,1,3} | broadcast | bytes 3932160 | tf_op jit(solution)/shard_map/broadcast_in_dim | solution.py:128
  94.0 3.1 %copy.49 = bf16[16,256,320]{1,2,0:T(8,128)(2,1)} copy(bf16[16,256,320]{2,0,1:T(8,128)(2,1)S(1)} %bitcast.79) | data formatting | bytes 5242880
  (33 shorter events, 0.3 us)
Async XLA Ops:
  7.2 4.7 %copy-start.2 = (s32[1280]{0:T(1024)S(1)}, s32[1280]{0:T(1024)}, u32[]{:S(2)}) copy-start(s32[1280]{0:T(1024)} %param.15) | copy-start | bytes 15364
  7.2 11.0 %copy-start.1 = (bf16[2,128,320]{1,2,0:T(8,128)(2,1)S(1)}, bf16[2,128,320]{1,2,0:T(8,128)(2,1)}, u32[]{:S(2)}) copy-start(bf16[2,128,320]{1,2,0:T(8,128)(2,1)} %param.17) | copy-start | bytes 491524
  7.2 30.2 %copy-start.8 = (f32[32]{0:T(128)S(1)}, f32[32]{0:T(128)}, u32[]{:S(2)}) copy-start(f32[32]{0:T(128)} %param.18) | copy-start | bytes 388
  7.2 30.2 %copy-start.6 = (f32[32]{0:T(128)S(1)}, f32[32]{0:T(128)}, u32[]{:S(2)}) copy-start(f32[32]{0:T(128)} %param.19) | copy-start | bytes 388
  7.2 30.2 %copy-start.7 = (f32[1,32]{1,0:T(1,128)S(1)}, f32[1,32]{1,0:T(1,128)}, u32[]{:S(2)}) copy-start(f32[1,32]{1,0:T(1,128)} %param.20) | copy-start | bytes 388
  7.2 30.2 %copy-start.5 = (f32[1,32]{1,0:T(1,128)S(1)}, f32[1,32]{1,0:T(1,128)}, u32[]{:S(2)}) copy-start(f32[1,32]{1,0:T(1,128)} %param.21) | copy-start | bytes 388
  7.2 42.7 %copy-start.4 = (f32[1280]{0:T(1024)S(1)}, f32[1280]{0:T(1024)}, u32[]{:S(2)}) copy-start(f32[1280]{0:T(1024)} %param.13) | copy-start | bytes 15364
  7.2 42.7 %copy-start.3 = (f32[1280]{0:T(1024)S(1)}, f32[1280]{0:T(1024)}, u32[]{:S(2)}) copy-start(f32[1280]{0:T(1024)} %param.14) | copy-start | bytes 15364
  7.2 54.3 %all-gather.2.cloned.1.call-start = ((), (), s32[]{:S(2)}) async-start(), calls=%async_computation.2 | async-start | bytes 3276800 | tf_op jit(solution)/shard_map/all_gather | solution.py:113
  12.8 9.2 %all-to-all-start = ((f32[4,1,64]{2,1,0:T(1,128)}), f32[4,1,64]{2,1,0:T(1,128)S(1)}, u32[]{:S(2)}, u32[]{:S(2)}) async-start(f32[4,1,64]{2,1,0:T(1,128)} %broadcast_in_dim.50), calls=%async_computation | async-start | bytes 4096 | tf_op jit(solution)/shard_map/all_to_all | solution.py:38
  18.2 19.1 %collective-permute-start = (bf16[1,128,320]{1,2,0:T(8,128)(2,1)S(1)}, bf16[1,128,320]{1,2,0:T(8,128)(2,1)S(1)}, u32[]{:S(2)}, u32[]{:S(2)}) collective-permute-start(bf16[1,128,320]{1,2,0:T(8,128)(2,1)S(1)} %get-tuple-element.43), channel_id=1, source_target_pairs={{0,4},{4,8},{8,12},{12,16},{16,20},{20,24},{24,28},{28,32},{32,36}... | collective-permute-start | bytes 245768 | tf_op jit(solution)/shard_map/ppermute | solution.py:58
  19.5 17.8 %collective-permute-start.1 = (bf16[1,128,320]{1,2,0:T(8,128)(2,1)S(1)}, bf16[1,128,320]{1,2,0:T(8,128)(2,1)S(1)}, u32[]{:S(2)}, u32[]{:S(2)}) collective-permute-start(bf16[1,128,320]{1,2,0:T(8,128)(2,1)S(1)} %get-tuple-element.44), channel_id=1, source_target_pairs={{4,0},{8,4},{12,8},{16,12},{20,16},{24,20},{28,24},{32,28},{36,32}... | collective-permute-start | bytes 245768 | tf_op jit(solution)/shard_map/ppermute | solution.py:61
  22.7 27.3 %all-to-all-start.1 = ((f32[64,1,64]{2,1,0:T(1,128)}), f32[64,1,64]{2,1,0:T(1,128)S(1)}, u32[]{:S(2)}, u32[]{:S(2)}) async-start(f32[64,1,64]{2,1,0:T(1,128)} %broadcast_in_dim.54), calls=%async_computation.1 | async-start | bytes 65536 | tf_op jit(solution)/shard_map/all_to_all | solution.py:38
  37.3 10.4 %collective-permute-start.2 = (bf16[1,2,128,320]{2,3,0,1:T(8,128)(2,1)S(1)}, bf16[1,2,128,320]{2,3,0,1:T(8,128)(2,1)S(1)}, u32[]{:S(2)}, u32[]{:S(2)}) collective-permute-start(bf16[1,2,128,320]{2,3,0,1:T(8,128)(2,1)S(1)} %maximum_bitcast_fusion.1), channel_id=1, source_target_pairs={{0,1},{1,0},{2,3},{3,2},{4,5},{5,4},{6,7},{7,6},{8,9},{9,8},{10,11... | collective-permute-start | bytes 491528 | tf_op jit(solution)/shard_map/ppermute | solution.py:21
  47.8 13.2 %collective-permute-start.3 = (bf16[2,2,128,320]{2,3,0,1:T(8,128)(2,1)S(1)}, bf16[2,2,128,320]{2,3,0,1:T(8,128)(2,1)S(1)}, u32[]{:S(2)}, u32[]{:S(2)}) collective-permute-start(bf16[2,2,128,320]{2,3,0,1:T(8,128)(2,1)S(1)} %pad_maximum_fusion), channel_id=1, source_target_pairs={{0,2},{1,3},{2,0},{3,1},{4,6},{5,7},{6,4},{7,5},{8,10},{9,11},{10,... | collective-permute-start | bytes 983048 | tf_op jit(solution)/shard_map/ppermute | solution.py:21
  77.8 4.7 %slice-start = ((s8[7372800]{0:T(1024)(128)(4,1)}), s8[3178496]{0:T(1024)(128)(4,1)S(1)}, s32[]{:S(2)}) async-start(s8[7372800]{0:T(1024)(128)(4,1)} %bitcast.94), calls=%async_computation.3 | async-start | bytes 6356992
  80.1 2.4 %slice-start.1 = ((s8[7372800]{0:T(1024)(128)(4,1)}), s8[4194304]{0:T(1024)(128)(4,1)S(1)}, s32[]{:S(2)}) async-start(s8[7372800]{0:T(1024)(128)(4,1)} %bitcast.94), calls=%async_computation.4 | async-start | bytes 8388608
  88.9 1.1 %copy-start = (bf16[8,128,320]{1,2,0:T(8,128)(2,1)S(1)}, bf16[8,128,320]{1,2,0:T(8,128)(2,1)}, u32[]{:S(2)}) copy-start(bf16[8,128,320]{1,2,0:T(8,128)(2,1)} %param.11) | copy-start | bytes 1966084
Sparse Core Ops, SparseCore 0:
  10.4 42.8 all-gather.1
